TPU v7x, 32 devices: a whole 2x2x4 slice. The times are simulated.
32 devices in a mesh: gx: 8 (over z, x), gy: 4 (over y, core).
Axes of the slice: x: 2, y: 2, z: 4, core: 2. Of those that a mesh axis runs over, the one named last changes fastest.
Arguments:
- measures: bfloat16 [262144, 128], P(('gx', 'gy')), may hold values from -6 to 6
- row_keys: int32 [262144], P(('gx', 'gy')), may hold values from 0 to 16383, as said below
- orders: bfloat16 [16384, 128], P(('gx', 'gy')), may hold values from -6 to 6
- heavy_keys: int32 [64], replicated, may hold values from 0 to 16383, as said below
- key_slot: int32 [16384], replicated, may hold values from 0 to 16383, as said below
Outputs:
- result: bfloat16 [16384, 128], P(('gx', 'gy'))
- heavy_report: bfloat16 [64, 128], P(('gx', 'gy'))
- slot_rows: float32 [16384], P(('gx', 'gy'))
Inputs may be any that keep to these rules, and one draw needn't show every extreme that they name: `heavy_keys`: for each range block d, entries d * 2 to (d + 1) * 2 - 1 are distinct keys of d * 512 to (d + 1) * 512 - 1. `key_slot`: A permutation. Slot s belongs to owner s // 2048 and to quarter (s // 512) % q with q = 4. Key k lies in range block d = k // 512; every range block has exactly 64 keys with slots of each owner, all in quarter d % q. `row_keys`: in the rows of one device, among rows whose key is not heavy, at most 768 have slots of any one owner and at most 192 distinct keys have slots of any one owner; in every device both bounds are reached by some owner.
All inputs are finite; a program needn't handle non-finite values.
Results may differ from a plain program's by a relative error of at most 0.0021.
Values may be sent and summed in bfloat16 or wider, within the bound.
A program may use at most 64 MiB of HBM per device.

v0:
```python
import jax
import jax.numpy as jnp
from jax import lax
from jax.sharding import PartitionSpec as P


def block_length(total):
    return 2048 if total % 2048 == 0 else total


def one_hot_sums(values, targets, labels, weights):
    block_rows = block_length(targets.shape[0])
    blocks = targets.shape[0] // block_rows
    columns = values.shape[1]
    span = labels.shape[0]
    exact = values.dtype == jnp.float32

    def add_block(running, block_piece):
        block_values, block_targets, block_weights = block_piece
        matches = block_targets[:, None] == labels[None, :]
        onehot = matches.astype(values.dtype)
        if exact:
            product = lax.dot_general(
                onehot,
                block_values,
                (((0,), (0,)), ((), ())),
                precision=lax.Precision.HIGHEST,
                preferred_element_type=jnp.float32,
            )
        else:
            product = lax.dot_general(
                onehot, block_values, (((0,), (0,)), ((), ())), preferred_element_type=jnp.float32
            )
        totals = running[0] + product
        tallies = running[1] + jnp.sum(matches.astype(jnp.float32) * block_weights[:, None], axis=0)
        return ((totals, tallies), jnp.any(matches, axis=1))

    start_state = (jnp.zeros((span, columns), jnp.float32), jnp.zeros((span,), jnp.float32))
    pieces = (
        values.reshape(blocks, block_rows, columns),
        targets.reshape(blocks, block_rows),
        weights.reshape(blocks, block_rows),
    )
    (totals, tallies), matched = lax.scan(add_block, start_state, pieces)
    return (totals, tallies, matched.reshape(-1))


def body(measures, row_keys, orders, heavy_keys, key_slot):
    row_count, columns = measures.shape
    groups_x = lax.axis_size("gx")
    groups_y = lax.axis_size("gy")
    key_dev = orders.shape[0]
    own_slots = key_dev * groups_y
    heavy_total = heavy_keys.shape[0]
    heavy_each = heavy_total // (groups_x * groups_y)
    capacity = max(row_count // 32, 3 * row_count // (4 * groups_x))
    key_capacity = capacity // 4
    index_x = lax.axis_index("gx")
    index_y = lax.axis_index("gy")
    device = index_x * groups_y + index_y
    unit_rows = jnp.ones((row_count,), jnp.float32)
    heavy_part, heavy_count, heavy_flags = one_hot_sums(measures, row_keys, heavy_keys, unit_rows)
    slot_ids = key_slot[row_keys]
    owner_labels = jnp.arange(groups_x + 1, dtype=jnp.int32)
    own_base = index_x * own_slots
    own_labels = jnp.arange(own_slots, dtype=jnp.int32)
    sort_keys = jnp.where(heavy_flags, groups_x * own_slots, slot_ids)
    ordering = jnp.argsort(sort_keys, stable=True)
    sorted_slots = sort_keys[ordering]
    sorted_owner = sorted_slots // own_slots
    is_light = sorted_owner < groups_x
    fresh = (
        jnp.concatenate([jnp.ones((1,), bool), sorted_slots[1:] != sorted_slots[:-1]]) & is_light
    )
    distinct = jnp.cumsum(fresh.astype(jnp.int32)) - 1
    before = jnp.sum(
        (fresh[:, None] & (sorted_owner[:, None] < owner_labels[None, :])).astype(jnp.int32), axis=0
    )
    segments = groups_x * key_capacity
    segment = jnp.where(
        is_light, sorted_owner * key_capacity + distinct - before[sorted_owner], segments
    )
    row_segment = jnp.zeros((row_count,), jnp.int32).at[ordering].set(segment)
    partial_value, tallies, unused = one_hot_sums(
        measures, row_segment, jnp.arange(segments, dtype=jnp.int32), unit_rows
    )
    sent_slots = jnp.full((segments + 1,), -1, jnp.int32).at[segment].set(sorted_slots)[:segments]
    got_sums, got_tallies, got_slots = (
        lax.all_to_all(
            partial_value.reshape(groups_x, key_capacity, columns),
            "gx",
            split_axis=0,
            concat_axis=0,
            tiled=True,
        ),
        lax.all_to_all(
            tallies.reshape(groups_x, key_capacity), "gx", split_axis=0, concat_axis=0, tiled=True
        ),
        lax.all_to_all(
            sent_slots.reshape(groups_x, key_capacity),
            "gx",
            split_axis=0,
            concat_axis=0,
            tiled=True,
        ),
    )
    local_slot = got_slots.reshape(-1) - own_base
    local_slot = jnp.where(got_slots.reshape(-1) >= 0, local_slot, own_slots)
    light_totals, light_tallies, unused_too = one_hot_sums(
        got_sums.reshape(-1, columns), local_slot, own_labels, got_tallies.reshape(-1)
    )
    quarter_totals, quarter_tallies = (
        lax.psum_scatter(
            light_totals.reshape(groups_y, key_dev, columns), "gy", scatter_dimension=0, tiled=True
        ),
        lax.psum_scatter(
            light_tallies.reshape(groups_y, key_dev), "gy", scatter_dimension=0, tiled=True
        ),
    )
    slot_rows = quarter_tallies.reshape(key_dev)
    inverse = jnp.argsort(key_slot)
    held_keys = lax.dynamic_slice_in_dim(inverse, device * key_dev, key_dev)
    send_order = jnp.argsort(held_keys)
    per_peer = key_dev // groups_x
    moved_totals, moved_tallies = (
        lax.all_to_all(
            quarter_totals.reshape(key_dev, columns)[send_order].reshape(
                groups_x, per_peer, columns
            ),
            "gx",
            split_axis=0,
            concat_axis=0,
            tiled=True,
        ),
        lax.all_to_all(
            slot_rows[send_order].reshape(groups_x, per_peer),
            "gx",
            split_axis=0,
            concat_axis=0,
            tiled=True,
        ),
    )
    range_slots = lax.dynamic_slice_in_dim(key_slot, device * key_dev, key_dev)
    arrival = jnp.argsort(range_slots // own_slots, stable=True)
    placed = jnp.argsort(arrival)
    light_sum = moved_totals.reshape(key_dev, columns)[placed]
    light_count = moved_tallies.reshape(key_dev)[placed]
    my_heavy = lax.dynamic_slice_in_dim(heavy_keys, device * heavy_each, heavy_each)
    heavy_local = my_heavy - device * key_dev
    heavy_orders_here = orders[heavy_local]
    gathered = lax.all_gather(heavy_orders_here, ("gx", "gy"), axis=0, tiled=True)
    joined = heavy_part * gathered.astype(jnp.float32)
    joined_total, count_total = lax.psum((joined, heavy_count), ("gx", "gy"))
    mine_joined = lax.dynamic_slice_in_dim(joined_total, device * heavy_each, heavy_each)
    mine_count = lax.dynamic_slice_in_dim(count_total, device * heavy_each, heavy_each)
    heavy_value = mine_joined * lax.rsqrt(1.0 + mine_count)[:, None]
    light_value = orders.astype(jnp.float32) * light_sum * lax.rsqrt(1.0 + light_count)[:, None]
    placing = (heavy_local[:, None] == jnp.arange(key_dev, dtype=jnp.int32)[None, :]).astype(
        jnp.float32
    )
    heavy_full = jnp.sum(placing[:, :, None] * heavy_value[:, None, :], axis=0)
    result = (light_value + heavy_full).astype(jnp.bfloat16)
    return (result, heavy_value.astype(jnp.bfloat16), slot_rows)


def solution(mesh):
    return jax.shard_map(
        body,
        mesh=mesh,
        in_specs=(P(("gx", "gy"), None), P(("gx", "gy")), P(("gx", "gy"), None), P(), P()),
        out_specs=(P(("gx", "gy"), None), P(("gx", "gy"), None), P(("gx", "gy"))),
        check_vma=False,
    )
```

profile of v0, /device:TPU:0, one launch (start us, length us, event | category | flops | bytes accessed | tf_op | source)
XLA Modules:
  0.0 408.1 jit_solution(12164380390125514987)
XLA Ops:
  8.8 12.8 %while.33 = (s32[]{:T(128)}, f32[64,128]{1,0:T(8,128)S(1)}, f32[64]{0:T(128)S(1)}, pred[4,2048]{1,0:T(4,128)(4,1)S(1)}, s32[4,2048]{1,0:T(4,128)S(1)}, /*index=5...) while((s32[]{:T(128)}, f32[64,128]{1,0:T(8,128)S(1)}, f32[64]{0:T(128)S(1)}, ...), condition=%wide.region_3.4_spmd.clone, body=%wide.region_0.3_spmd.clone.sunk | while | flops 34355264 | bytes 643696 | solution.py:44
  21.6 45.5 %gather_fusion = s32[8192]{0:T(1024)S(1)} fusion(s32[16384]{0:T(1024)S(1)} %copy-done, s32[8192]{0:T(1024)S(1)} %fusion.26), kind=kCustom, calls=%fused_computation | custom fusion | bytes 98304 | tf_op jit(solution)/shard_map/gather | solution.py:63
  67.2 6.8 %sort.82 = (s32[8192]{0:T(1024)}, s32[8192]{0:T(1024)S(1)}) sort(s32[8192]{0:T(1024)S(1)} %broadcast_select_fusion.1, s32[8192]{0:T(1024)S(1)} %iota.43), dimensions={0}, to_apply=%region_4.5 | sort | flops 106496 | bytes 131072 | tf_op jit(solution)/shard_map/jit(argsort)/sort | solution.py:68
  73.9 45.5 %gather_fusion.1 = s32[8192]{0:T(1024)S(1)} fusion(s32[8192]{0:T(1024)S(1)} %broadcast_select_fusion.1, s32[8192]{0:T(1024)S(1)} %get-tuple-element.195), kind=kCustom, calls=%fused_computation.1 | custom fusion | bytes 98304 | tf_op jit(solution)/shard_map/gather | solution.py:69
  120.6 4.7 %compare_select_fusion.3 = (s32[8192,1]{0,1:T(1,128)S(1)}, s32[8192,1]{0,1:T(1,128)S(1)}, s32[8192,1]{0,1:T(1,128)S(1)}) fusion(s32[]{:T(128)} %bitcast.7, s32[]{:T(128)} %bitcast.8, s32[]{:T(128)} %bitcast.9, s32[]{:T(128)} %bitcast.10, s32[]{:T(128)} %bitcast.11, s32[]{:T(128)} %bitcast.13, s32[]{:T(128)} %bitcast.12, s32[8192,1]{0,1:T(1,128)S(1)} %bitcast.83), kind=kLoop, calls=%fused_computation.49 | loop fusion | flops 245760 | bytes 131100 | tf_op jit(solution)/shard_map/gather | solution.py:81
  127.5 30.4 %scatter_custom_fusion = s32[1537]{0:T(1024)S(1)} fusion(s32[8192]{0:T(1024)S(1)} %bitcast.93, s32[8192]{0:T(1024)S(1)} %gather_fusion.1, s32[]{:T(128)} %constant.66.clone.1), kind=kCustom, calls=%fused_computation.106 | custom fusion | bytes 6152 | tf_op jit(solution)/shard_map/scatter | solution.py:87
  158.7 7.3 %all-to-all-start = ((s32[8,1,192]{2,1,0:T(1,128)}), s32[8,1,192]{2,1,0:T(1,128)S(1)}, u32[]{:S(2)}, u32[]{:S(2)}) async-start(s32[8,1,192]{2,1,0:T(1,128)} %all_to_all.24), calls=%async_computation | async-start | bytes 16384 | tf_op jit(solution)/shard_map/all_to_all | solution.py:99
  165.9 30.7 %scatter_custom_fusion.1 = s32[8192]{0:T(1024)S(1)} fusion(s32[8192]{0:T(1024)S(1)} %get-tuple-element.196, s32[8192]{0:T(1024)S(1)} %get-tuple-element.185, s32[]{:T(128)} %constant.68.clone.1), kind=kCustom, calls=%fused_computation.95 | custom fusion | bytes 32772 | tf_op jit(solution)/shard_map/scatter | solution.py:83
  196.6 30.3 %while.34 = (s32[]{:T(128)}, f32[1536,128]{1,0:T(8,128)}, f32[1536]{0:T(1024)S(1)}, s32[4,2048]{1,0:T(4,128)S(1)}, bf16[4,2048,128]{2,1,0:T(8,128)(2,1)}, /*index=5*/s32[]{:T(128)}, s32[]{:T(128)}) while((s32[]{:T(128)}, f32[1536,128]{1,0:T(8,128)}, f32[1536]{0:T(1024)S(1)}, s32[4,2048]{1,0:T(4,128)S(1)}, ...), condition=%wide.region_12.13_spmd.clone, body=%wide.region_10.12_spmd.clone.sunk | while | flops 818284032 | bytes 2155100 | solution.py:44
  196.7 5.7 %fusion.56 = f32[1536,128]{1,0:T(8,128)} fusion(s32[2048]{0:T(1024)S(1)} %bitcast.85, f32[1536,128]{1,0:T(8,128)} %get-tuple-element.315, bf16[4,2048,128]{2,1,0:T(8,128)(2,1)} %get-tuple-element.325, s32[]{:T(128)} %get-tuple-element.314, pred[]{:T(512)S(6)} %compare.110), kind=kOutput, calls=%fused_computation.28.clone.1 | convolution fusion | flops 808845312 | bytes 2105857 | tf_op jit(solution)/shard_map/while/body/eval_jaxpr/dot_general | solution.py:31
  204.1 5.9 %fusion.56 = f32[1536,128]{1,0:T(8,128)} fusion(s32[2048]{0:T(1024)S(1)} %bitcast.85, f32[1536,128]{1,0:T(8,128)} %get-tuple-element.315, bf16[4,2048,128]{2,1,0:T(8,128)(2,1)} %get-tuple-element.325, s32[]{:T(128)} %get-tuple-element.314, pred[]{:T(512)S(6)} %compare.110), kind=kOutput, calls=%fused_computation.28.clone.1 | convolution fusion | flops 808845312 | bytes 2105857 | tf_op jit(solution)/shard_map/while/body/eval_jaxpr/dot_general | solution.py:31
  211.7 5.9 %fusion.56 = f32[1536,128]{1,0:T(8,128)} fusion(s32[2048]{0:T(1024)S(1)} %bitcast.85, f32[1536,128]{1,0:T(8,128)} %get-tuple-element.315, bf16[4,2048,128]{2,1,0:T(8,128)(2,1)} %get-tuple-element.325, s32[]{:T(128)} %get-tuple-element.314, pred[]{:T(512)S(6)} %compare.110), kind=kOutput, calls=%fused_computation.28.clone.1 | convolution fusion | flops 808845312 | bytes 2105857 | tf_op jit(solution)/shard_map/while/body/eval_jaxpr/dot_general | solution.py:31
  219.3 5.9 %fusion.56 = f32[1536,128]{1,0:T(8,128)} fusion(s32[2048]{0:T(1024)S(1)} %bitcast.85, f32[1536,128]{1,0:T(8,128)} %get-tuple-element.315, bf16[4,2048,128]{2,1,0:T(8,128)(2,1)} %get-tuple-element.325, s32[]{:T(128)} %get-tuple-element.314, pred[]{:T(512)S(6)} %compare.110), kind=kOutput, calls=%fused_computation.28.clone.1 | convolution fusion | flops 808845312 | bytes 2105857 | tf_op jit(solution)/shard_map/while/body/eval_jaxpr/dot_general | solution.py:31
  226.9 6.0 %all-to-all-start.1 = ((f32[8,192,128]{2,1,0:T(8,128)}), f32[8,192,128]{2,1,0:T(8,128)S(1)}, u32[]{:S(2)}, u32[]{:S(2)}) async-start(f32[8,192,128]{2,1,0:T(8,128)} %bitcast.18), calls=%async_computation.1 | async-start | bytes 1572864 | tf_op jit(solution)/shard_map/all_to_all | solution.py:89
  233.1 19.5 %all-to-all-done.1 = f32[8,192,128]{2,1,0:T(8,128)S(1)} async-done(((f32[8,192,128]{2,1,0:T(8,128)}), f32[8,192,128]{2,1,0:T(8,128)S(1)}, u32[]{:S(2)}, u32[]{:S(2)}) %all-to-all-start.1) | async-done | bytes 786464 | tf_op jit(solution)/shard_map/all_to_all | solution.py:89
  252.6 6.3 %fusion.18 = f32[4,512,128]{2,1,0:T(8,128)} fusion(f32[1536,128,1]{1,0,2:T(8,128)S(1)} %bitcast.84, s32[4,512]{1,0:T(4,128)S(1)} %multiply_add_fusion, s32[1536]{0:T(1024)S(1)} %select_n.113), kind=kOutput, calls=%fused_computation.36 | convolution fusion | flops 4834983936 | bytes 1849344 | tf_op jit(solution)/shard_map/while/body/eval_jaxpr/dot_general | solution.py:23
  259.6 3.5 all-to-all-start.3
  263.1 7.8 %sort.83 = (s32[16384]{0:T(1024)}, s32[16384]{0:T(1024)S(1)}) sort(s32[16384]{0:T(1024)S(1)} %copy-done, s32[16384]{0:T(1024)S(1)} %iota.45), dimensions={0}, to_apply=%region_14.15 | sort | flops 229376 | bytes 262144 | tf_op jit(solution)/shard_map/jit(argsort)/sort | solution.py:121
  271.5 3.8 sort.84
  275.4 3.8 sort.85
  279.2 3.8 sort.86
  283.6 42.0 %all-gather.1 = bf16[32,2,128]{2,1,0:T(2,128)(2,1)S(1)} all-gather(bf16[1,2,128]{2,1,0:T(2,128)(2,1)S(1)} %bitcast.95), channel_id=2, replica_groups=mesh['gx'=8,'gy'=4] {'gx','gy'}, dimensions={0}, use_global_device_ids=true | all-gather | bytes 16896 | tf_op jit(solution)/shard_map/all_gather | solution.py:151
  325.7 37.2 %all-reduce.1 = (f32[64,128]{1,0:T(8,128)S(1)}, f32[64]{0:T(128)S(1)}) all-reduce(f32[64,128]{1,0:T(8,128)S(1)} %convert_multiply_fusion, f32[64]{0:T(128)S(1)} %get-tuple-element.110), channel_id=1, replica_groups=mesh['gx'=8,'gy'=4] {'gx','gy'}, use_global_device_ids=true, to_apply=%region_20.21 | all-reduce | flops 8256 | bytes 66048 | tf_op jit(solution)/shard_map/psum | solution.py:153
  362.9 1.8 select_reduce_fusion
  364.8 5.9 %all-reduce = f32[4,512]{1,0:T(4,128)S(1)} all-reduce(f32[4,512]{1,0:T(4,128)S(1)} %reshape.288), channel_id=4, replica_groups=mesh['gx'=8,'gy'=4] {'gy'}, use_global_device_ids=true, to_apply=%region_19.20.clone | all-reduce | flops 2048 | bytes 16384
  371.4 3.5 gather_fusion.4
  375.5 5.9 %all-to-all-start.4 = ((f32[8,1,64]{2,1,0:T(1,128)}), f32[8,1,64]{2,1,0:T(1,128)S(1)}, u32[]{:S(2)}, u32[]{:S(2)}) async-start(f32[8,1,64]{2,1,0:T(1,128)} %all_to_all.30), calls=%async_computation.5 | async-start | bytes 8192 | tf_op jit(solution)/shard_map/all_to_all | solution.py:135
  381.5 2.6 gather_fusion.2
  384.1 3.7 all-to-all-done.4
  387.8 3.4 all-to-all-start.2
  393.3 3.5 gather_fusion.5
  396.8 2.6 all-to-all-done.2
  (114 shorter events, 32.6 us)
Async XLA Ops:
  7.2 14.4 %copy-start = (s32[16384]{0:T(1024)S(1)}, s32[16384]{0:T(1024)}, u32[]{:S(2)}) copy-start(s32[16384]{0:T(1024)} %param.13) | copy-start | bytes 196612
  158.7 68.2 %all-to-all-start = ((s32[8,1,192]{2,1,0:T(1,128)}), s32[8,1,192]{2,1,0:T(1,128)S(1)}, u32[]{:S(2)}, u32[]{:S(2)}) async-start(s32[8,1,192]{2,1,0:T(1,128)} %all_to_all.24), calls=%async_computation | async-start | bytes 16384 | tf_op jit(solution)/shard_map/all_to_all | solution.py:99
  226.9 25.7 %all-to-all-start.1 = ((f32[8,192,128]{2,1,0:T(8,128)}), f32[8,192,128]{2,1,0:T(8,128)S(1)}, u32[]{:S(2)}, u32[]{:S(2)}) async-start(f32[8,192,128]{2,1,0:T(8,128)} %bitcast.18), calls=%async_computation.1 | async-start | bytes 1572864 | tf_op jit(solution)/shard_map/all_to_all | solution.py:89
  232.9 148.6 %reduce-scatter.2.cloned.1.call-start = ((), (), s32[]{:S(2)}) async-start(), calls=%async_computation.6 | async-start | bytes 1310720 | tf_op jit(solution)/shard_map/reduce_scatter | solution.py:113
  252.6 18.3 %copy-start.4 = (u32[32]{0:T(128)S(1)}, u32[32]{0:T(128)}, u32[]{:S(2)}) copy-start(u32[32]{0:T(128)} %constant.146) | copy-start | bytes 388
  252.6 30.3 %copy-start.3 = (s32[64]{0:T(128)S(1)}, s32[64]{0:T(128)}, u32[]{:S(2)}) copy-start(s32[64]{0:T(128)} %get-tuple-element.335) | copy-start | bytes 772
  252.6 30.4 %copy-start.2 = (bf16[512,128]{1,0:T(8,128)(2,1)S(1)}, bf16[512,128]{1,0:T(8,128)(2,1)}, u32[]{:S(2)}) copy-start(bf16[512,128]{1,0:T(8,128)(2,1)} %param.11) | copy-start | bytes 393220
  259.6 103.3 %all-to-all-start.3 = ((f32[8,1,192]{2,1,0:T(1,128)}), f32[8,1,192]{2,1,0:T(1,128)S(1)}, u32[]{:S(2)}, u32[]{:S(2)}) async-start(f32[8,1,192]{2,1,0:T(1,128)} %all_to_all.28), calls=%async_computation.4 | async-start | bytes 16384 | tf_op jit(solution)/shard_map/all_to_all | solution.py:96
  371.3 12.7 %copy-start.1 = (f32[1,512]{1,0:T(1,128)}, f32[1,512]{1,0:T(1,128)S(1)}, u32[]{:S(2)}) copy-start(f32[1,512]{1,0:T(1,128)S(1)} %constant_dynamic-slice_fusion.2) | copy-start | bytes 6148
  375.5 12.3 %all-to-all-start.4 = ((f32[8,1,64]{2,1,0:T(1,128)}), f32[8,1,64]{2,1,0:T(1,128)S(1)}, u32[]{:S(2)}, u32[]{:S(2)}) async-start(f32[8,1,64]{2,1,0:T(1,128)} %all_to_all.30), calls=%async_computation.5 | async-start | bytes 8192 | tf_op jit(solution)/shard_map/all_to_all | solution.py:135
  387.8 11.6 %all-to-all-start.2 = ((f32[8,64,128]{2,1,0:T(8,128)}), f32[8,64,128]{2,1,0:T(8,128)S(1)}, u32[]{:S(2)}, u32[]{:S(2)}) async-start(f32[8,64,128]{2,1,0:T(8,128)} %bitcast.22), calls=%async_computation.3 | async-start | bytes 524288 | tf_op jit(solution)/shard_map/all_to_all | solution.py:126
Sparse Core Ops, SparseCore 0:
  259.0 23.9 reduce-scatter.1
where the time goes:
time: 409 us; the launch traced here: 408 us
  local copies, waits for them, and re-layouts  170 us (42%)
  blocking collectives  85 us (21%)
  other arithmetic  51.7 us (13%)
  matrix products  35 us (9%)
  starting transfers between devices  26.1 us (6%)
  waiting for transfers between devices  25.9 us (6%)
  between operations  14.4 us (4%)
    gather x1, local copies, waits for them, and re-layouts, body(): slot_ids = key_slot[row_keys]  45.5 us
    gather x1, local copies, waits for them, and re-layouts, body(): sorted_slots = sort_keys[ordering]  45.5 us
    all_gather x1, blocking collectives, body(): lax.all_gather(heavy_orders_here, ('gx', 'gy'), axis=0, tiled=True)  42 us
    psum x1, blocking collectives, body(): joined_total, count_total = lax.psum((joined, heavy_count), ('gx', 'gy'))  37.2 us
    scatter x1, local copies, waits for them, and re-layouts, body(): row_segment = jnp.zeros((row_count,), jnp.int32).at[ordering].set(segment)  30.7 us
    scatter x1, local copies, waits for them, and re-layouts, body(): jnp.full((segments + 1,), -1, jnp.int32).at[segment].set(sorted_slots)  30.4 us
    dot_general x8, matrix products, add_block(): lax.dot_general(onehot, block_values, (((0,), (0,)), ((), ())), preferred...  28.7 us
    all_to_all x1, waiting for transfers between devices, body(): lax.all_to_all(partial_value.reshape(groups_x, key_capacity, columns), 'g...  19.5 us
  transfers between devices with their start and end apart: 6, of which 3 were waited for; matrix products, arithmetic and copies ran while one was open for 23% of the time, Pallas kernels for 0%

commit v1 on v0

--- a/solution.py
+++ b/solution.py
@@ -148,7 +148,16 @@
     my_heavy = lax.dynamic_slice_in_dim(heavy_keys, device * heavy_each, heavy_each)
     heavy_local = my_heavy - device * key_dev
     heavy_orders_here = orders[heavy_local]
-    gathered = lax.all_gather(heavy_orders_here, ("gx", "gy"), axis=0, tiled=True)
+    bring_scales = lambda obj, dim_at: jnp.concatenate(
+        lax.all_to_all(
+            jnp.stack([obj for _ in range(lax.axis_size(("gx", "gy")))]),
+            axis_name=("gx", "gy"),
+            split_axis=0,
+            concat_axis=0,
+        ),
+        axis=dim_at,
+    )
+    gathered = bring_scales(heavy_orders_here, dim_at=0)
     joined = heavy_part * gathered.astype(jnp.float32)
     joined_total, count_total = lax.psum((joined, heavy_count), ("gx", "gy"))
     mine_joined = lax.dynamic_slice_in_dim(joined_total, device * heavy_each, heavy_each)

time: 409 us -> 359 us (0.88)
  blocking collectives: 85 us -> 46.9 us
  waiting for transfers between devices: 25.9 us -> 8.2 us
  starting transfers between devices: 26.1 us -> 31.3 us
    all_gather x1 -> x0, blocking collectives: 42 us -> none  [body(): lax.all_gather(heavy_orders_here, ('gx', 'gy'), axis=0, tiled=True)]
    all_to_all x1, waiting for transfers between devices: 19.5 us -> 0.01 us  [body(): lax.all_to_all(partial_value.reshape(groups_x, key_capacity, columns), 'g...]
  transfers between devices with their start and end apart: 6 -> 7, of which waited for: 3 -> 2; matrix products, arithmetic and copies ran while one was open for 23% -> 28% of each run, Pallas kernels for 0% -> 0%
where the time goes in v1:
time: 359 us; the launch traced here: 358 us
  local copies, waits for them, and re-layouts  170 us (47%)
  other arithmetic  51.7 us (14%)
  blocking collectives  46.9 us (13%)
  matrix products  35 us (10%)
  starting transfers between devices  31.3 us (9%)
  between operations  14.4 us (4%)
  waiting for transfers between devices  8.2 us (2%)
    gather x1, local copies, waits for them, and re-layouts, body(): slot_ids = key_slot[row_keys]  45.5 us
    gather x1, local copies, waits for them, and re-layouts, body(): sorted_slots = sort_keys[ordering]  45.5 us
    psum x1, blocking collectives, body(): joined_total, count_total = lax.psum((joined, heavy_count), ('gx', 'gy'))  41.1 us
    scatter x1, local copies, waits for them, and re-layouts, body(): row_segment = jnp.zeros((row_count,), jnp.int32).at[ordering].set(segment)  30.7 us
    scatter x1, local copies, waits for them, and re-layouts, body(): jnp.full((segments + 1,), -1, jnp.int32).at[segment].set(sorted_slots)  30.4 us
    dot_general x8, matrix products, add_block(): lax.dot_general(onehot, block_values, (((0,), (0,)), ((), ())), preferred...  28.7 us
    reduce_sum x9, other arithmetic, add_block(): jnp.sum(matches.astype(jnp.float32) * block_weights[:, None], axis=0)  12 us
    sort x1, other arithmetic, body(): inverse = jnp.argsort(key_slot)  7.75 us
  transfers between devices with their start and end apart: 7, of which 2 were waited for; matrix products, arithmetic and copies ran while one was open for 28% of the time, Pallas kernels for 0%

profile of v1, /device:TPU:0, one launch (start us, length us, event | category | flops | bytes accessed | tf_op | source)
XLA Modules:
  0.0 358.1 jit_solution(13248596491475661887)
XLA Ops:
  8.8 12.8 %while.33 = (s32[]{:T(128)}, f32[64,128]{1,0:T(8,128)S(1)}, f32[64]{0:T(128)S(1)}, pred[4,2048]{1,0:T(4,128)(4,1)S(1)}, s32[4,2048]{1,0:T(4,128)S(1)}, /*index=5...) while((s32[]{:T(128)}, f32[64,128]{1,0:T(8,128)S(1)}, f32[64]{0:T(128)S(1)}, ...), condition=%wide.region_3.4_spmd.clone, body=%wide.region_0.3_spmd.clone.sunk | while | flops 34355264 | bytes 643696 | solution.py:44
  21.6 45.5 %gather_fusion = s32[8192]{0:T(1024)S(1)} fusion(s32[16384]{0:T(1024)S(1)} %copy-done, s32[8192]{0:T(1024)S(1)} %fusion.26), kind=kCustom, calls=%fused_computation | custom fusion | bytes 98304 | tf_op jit(solution)/shard_map/gather | solution.py:63
  67.2 6.8 %sort.82 = (s32[8192]{0:T(1024)}, s32[8192]{0:T(1024)S(1)}) sort(s32[8192]{0:T(1024)S(1)} %broadcast_select_fusion.1, s32[8192]{0:T(1024)S(1)} %iota.43), dimensions={0}, to_apply=%region_4.5 | sort | flops 106496 | bytes 131072 | tf_op jit(solution)/shard_map/jit(argsort)/sort | solution.py:68
  73.9 45.5 %gather_fusion.1 = s32[8192]{0:T(1024)S(1)} fusion(s32[8192]{0:T(1024)S(1)} %broadcast_select_fusion.1, s32[8192]{0:T(1024)S(1)} %get-tuple-element.195), kind=kCustom, calls=%fused_computation.1 | custom fusion | bytes 98304 | tf_op jit(solution)/shard_map/gather | solution.py:69
  120.6 4.7 %compare_select_fusion.3 = (s32[8192,1]{0,1:T(1,128)S(1)}, s32[8192,1]{0,1:T(1,128)S(1)}, s32[8192,1]{0,1:T(1,128)S(1)}) fusion(s32[]{:T(128)} %bitcast.7, s32[]{:T(128)} %bitcast.8, s32[]{:T(128)} %bitcast.9, s32[]{:T(128)} %bitcast.10, s32[]{:T(128)} %bitcast.11, s32[]{:T(128)} %bitcast.13, s32[]{:T(128)} %bitcast.12, s32[8192,1]{0,1:T(1,128)S(1)} %bitcast.82), kind=kLoop, calls=%fused_computation.49 | loop fusion | flops 245760 | bytes 131100 | tf_op jit(solution)/shard_map/gather | solution.py:81
  127.5 30.4 %scatter_custom_fusion = s32[1537]{0:T(1024)S(1)} fusion(s32[8192]{0:T(1024)S(1)} %bitcast.92, s32[8192]{0:T(1024)S(1)} %gather_fusion.1, s32[]{:T(128)} %constant.66.clone.1), kind=kCustom, calls=%fused_computation.106 | custom fusion | bytes 6152 | tf_op jit(solution)/shard_map/scatter | solution.py:87
  158.7 7.3 %all-to-all-start = ((s32[8,1,192]{2,1,0:T(1,128)}), s32[8,1,192]{2,1,0:T(1,128)S(1)}, u32[]{:S(2)}, u32[]{:S(2)}) async-start(s32[8,1,192]{2,1,0:T(1,128)} %all_to_all.27), calls=%async_computation | async-start | bytes 16384 | tf_op jit(solution)/shard_map/all_to_all | solution.py:99
  165.9 30.7 %scatter_custom_fusion.1 = s32[8192]{0:T(1024)S(1)} fusion(s32[8192]{0:T(1024)S(1)} %get-tuple-element.196, s32[8192]{0:T(1024)S(1)} %get-tuple-element.185, s32[]{:T(128)} %constant.68.clone.1), kind=kCustom, calls=%fused_computation.95 | custom fusion | bytes 32772 | tf_op jit(solution)/shard_map/scatter | solution.py:83
  196.6 30.3 %while.34 = (s32[]{:T(128)}, f32[1536,128]{1,0:T(8,128)}, f32[1536]{0:T(1024)S(1)}, s32[4,2048]{1,0:T(4,128)S(1)}, bf16[4,2048,128]{2,1,0:T(8,128)(2,1)}, /*index=5*/s32[]{:T(128)}, s32[]{:T(128)}) while((s32[]{:T(128)}, f32[1536,128]{1,0:T(8,128)}, f32[1536]{0:T(1024)S(1)}, s32[4,2048]{1,0:T(4,128)S(1)}, ...), condition=%wide.region_12.13_spmd.clone, body=%wide.region_10.12_spmd.clone.sunk | while | flops 818284032 | bytes 2155100 | solution.py:44
  196.7 5.7 %fusion.56 = f32[1536,128]{1,0:T(8,128)} fusion(s32[2048]{0:T(1024)S(1)} %bitcast.84, f32[1536,128]{1,0:T(8,128)} %get-tuple-element.315, bf16[4,2048,128]{2,1,0:T(8,128)(2,1)} %get-tuple-element.325, s32[]{:T(128)} %get-tuple-element.314, pred[]{:T(512)S(6)} %compare.110), kind=kOutput, calls=%fused_computation.28.clone.1 | convolution fusion | flops 808845312 | bytes 2105857 | tf_op jit(solution)/shard_map/while/body/eval_jaxpr/dot_general | solution.py:31
  202.3 1.7 fusion.57
  204.1 5.9 %fusion.56 = f32[1536,128]{1,0:T(8,128)} fusion(s32[2048]{0:T(1024)S(1)} %bitcast.84, f32[1536,128]{1,0:T(8,128)} %get-tuple-element.315, bf16[4,2048,128]{2,1,0:T(8,128)(2,1)} %get-tuple-element.325, s32[]{:T(128)} %get-tuple-element.314, pred[]{:T(512)S(6)} %compare.110), kind=kOutput, calls=%fused_computation.28.clone.1 | convolution fusion | flops 808845312 | bytes 2105857 | tf_op jit(solution)/shard_map/while/body/eval_jaxpr/dot_general | solution.py:31
  211.7 5.9 %fusion.56 = f32[1536,128]{1,0:T(8,128)} fusion(s32[2048]{0:T(1024)S(1)} %bitcast.84, f32[1536,128]{1,0:T(8,128)} %get-tuple-element.315, bf16[4,2048,128]{2,1,0:T(8,128)(2,1)} %get-tuple-element.325, s32[]{:T(128)} %get-tuple-element.314, pred[]{:T(512)S(6)} %compare.110), kind=kOutput, calls=%fused_computation.28.clone.1 | convolution fusion | flops 808845312 | bytes 2105857 | tf_op jit(solution)/shard_map/while/body/eval_jaxpr/dot_general | solution.py:31
  219.3 5.9 %fusion.56 = f32[1536,128]{1,0:T(8,128)} fusion(s32[2048]{0:T(1024)S(1)} %bitcast.84, f32[1536,128]{1,0:T(8,128)} %get-tuple-element.315, bf16[4,2048,128]{2,1,0:T(8,128)(2,1)} %get-tuple-element.325, s32[]{:T(128)} %get-tuple-element.314, pred[]{:T(512)S(6)} %compare.110), kind=kOutput, calls=%fused_computation.28.clone.1 | convolution fusion | flops 808845312 | bytes 2105857 | tf_op jit(solution)/shard_map/while/body/eval_jaxpr/dot_general | solution.py:31
  226.9 6.0 %all-to-all-start.1 = ((f32[8,192,128]{2,1,0:T(8,128)}), f32[8,192,128]{2,1,0:T(8,128)S(1)}, u32[]{:S(2)}, u32[]{:S(2)}) async-start(f32[8,192,128]{2,1,0:T(8,128)} %bitcast.18), calls=%async_computation.1 | async-start | bytes 1572864 | tf_op jit(solution)/shard_map/all_to_all | solution.py:89
  233.6 7.7 %sort.83 = (s32[16384]{0:T(1024)}, s32[16384]{0:T(1024)S(1)}) sort(s32[16384]{0:T(1024)S(1)} %copy-done, s32[16384]{0:T(1024)S(1)} %iota.45), dimensions={0}, to_apply=%region_14.15 | sort | flops 229376 | bytes 262144 | tf_op jit(solution)/shard_map/jit(argsort)/sort | solution.py:121
  241.4 3.8 %sort.84 = (s32[512]{0:T(512)}, s32[512]{0:T(512)S(1)}) sort(s32[512]{0:T(512)S(1)} %dynamic_slice.41, s32[512]{0:T(512)S(1)} %iota.46), dimensions={0}, to_apply=%region_15.16 | sort | flops 4608 | bytes 8192 | tf_op jit(solution)/shard_map/jit(argsort)/sort | solution.py:123
  245.3 3.8 %sort.85 = (s32[512]{0:T(512)}, s32[512]{0:T(512)S(1)}) sort(s32[512]{0:T(512)S(1)} %add_select_fusion.2, s32[512]{0:T(512)S(1)} %iota.47), dimensions={0}, to_apply=%region_16.17 | sort | flops 4608 | bytes 8192 | tf_op jit(solution)/shard_map/jit(argsort)/sort | solution.py:144
  249.1 3.8 %sort.86 = (s32[512]{0:T(512)}, s32[512]{0:T(512)S(1)}) sort(s32[512]{0:T(512)S(1)} %get-tuple-element.106, s32[512]{0:T(512)S(1)} %iota.48), dimensions={0}, to_apply=%region_17.18 | sort | flops 4608 | bytes 8192 | tf_op jit(solution)/shard_map/jit(argsort)/sort | solution.py:145
  252.9 6.0 %all-to-all-start.3 = ((f32[8,1,192]{2,1,0:T(1,128)}), f32[8,1,192]{2,1,0:T(1,128)S(1)}, u32[]{:S(2)}, u32[]{:S(2)}) async-start(f32[8,1,192]{2,1,0:T(1,128)} %all_to_all.31), calls=%async_computation.4 | async-start | bytes 16384 | tf_op jit(solution)/shard_map/all_to_all | solution.py:96
  259.2 6.3 %fusion.18 = f32[4,512,128]{2,1,0:T(8,128)} fusion(f32[1536,128,1]{1,0,2:T(8,128)S(1)} %bitcast.83, s32[4,512]{1,0:T(4,128)S(1)} %multiply_add_fusion, s32[1536]{0:T(1024)S(1)} %select_n.113), kind=kOutput, calls=%fused_computation.36 | convolution fusion | flops 4834983936 | bytes 1849344 | tf_op jit(solution)/shard_map/while/body/eval_jaxpr/dot_general | solution.py:23
  266.4 1.8 select_reduce_fusion
  268.3 5.8 %all-reduce = f32[4,512]{1,0:T(4,128)S(1)} all-reduce(f32[4,512]{1,0:T(4,128)S(1)} %reshape.293), channel_id=3, replica_groups=mesh['gx'=8,'gy'=4] {'gy'}, use_global_device_ids=true, to_apply=%region_19.20.clone | all-reduce | flops 2048 | bytes 16384
  274.7 3.5 gather_fusion.4
  278.9 5.7 %all-to-all-start.4 = ((f32[8,1,64]{2,1,0:T(1,128)}), f32[8,1,64]{2,1,0:T(1,128)S(1)}, u32[]{:S(2)}, u32[]{:S(2)}) async-start(f32[8,1,64]{2,1,0:T(1,128)} %all_to_all.33), calls=%async_computation.5 | async-start | bytes 8192 | tf_op jit(solution)/shard_map/all_to_all | solution.py:135
  285.2 5.8 %all-to-all-done.4 = f32[8,1,64]{2,1,0:T(1,128)S(1)} async-done(((f32[8,1,64]{2,1,0:T(1,128)}), f32[8,1,64]{2,1,0:T(1,128)S(1)}, u32[]{:S(2)}, u32[]{:S(2)}) %all-to-all-start.4) | async-done | bytes 2080 | tf_op jit(solution)/shard_map/all_to_all | solution.py:135
  291.6 2.5 all-to-all-start.5
  295.5 3.5 gather_fusion.5
  299.0 2.3 all-to-all-done.5
  301.3 2.6 gather_fusion.2
  303.9 3.5 all-to-all-start.2
  307.4 41.1 %all-reduce.1 = (f32[64,128]{1,0:T(8,128)S(1)}, f32[64]{0:T(128)S(1)}) all-reduce(f32[64,128]{1,0:T(8,128)S(1)} %convert_multiply_fusion, f32[64]{0:T(128)S(1)} %get-tuple-element.110), channel_id=1, replica_groups=mesh['gx'=8,'gy'=4] {'gx','gy'}, use_global_device_ids=true, to_apply=%region_20.21 | all-reduce | flops 8256 | bytes 66048 | tf_op jit(solution)/shard_map/psum | solution.py:162
  (116 shorter events, 31.8 us)
Async XLA Ops:
  7.2 14.4 %copy-start = (s32[16384]{0:T(1024)S(1)}, s32[16384]{0:T(1024)}, u32[]{:S(2)}) copy-start(s32[16384]{0:T(1024)} %param.13) | copy-start | bytes 196612
  158.7 68.2 %all-to-all-start = ((s32[8,1,192]{2,1,0:T(1,128)}), s32[8,1,192]{2,1,0:T(1,128)S(1)}, u32[]{:S(2)}, u32[]{:S(2)}) async-start(s32[8,1,192]{2,1,0:T(1,128)} %all_to_all.27), calls=%async_computation | async-start | bytes 16384 | tf_op jit(solution)/shard_map/all_to_all | solution.py:99
  226.9 26.0 %all-to-all-start.1 = ((f32[8,192,128]{2,1,0:T(8,128)}), f32[8,192,128]{2,1,0:T(8,128)S(1)}, u32[]{:S(2)}, u32[]{:S(2)}) async-start(f32[8,192,128]{2,1,0:T(8,128)} %bitcast.18), calls=%async_computation.1 | async-start | bytes 1572864 | tf_op jit(solution)/shard_map/all_to_all | solution.py:89
  252.9 13.4 %all-to-all-start.3 = ((f32[8,1,192]{2,1,0:T(1,128)}), f32[8,1,192]{2,1,0:T(1,128)S(1)}, u32[]{:S(2)}, u32[]{:S(2)}) async-start(f32[8,1,192]{2,1,0:T(1,128)} %all_to_all.31), calls=%async_computation.4 | async-start | bytes 16384 | tf_op jit(solution)/shard_map/all_to_all | solution.py:96
  258.9 42.4 %reduce-scatter.2.cloned.1.call-start = ((), (), s32[]{:S(2)}) async-start(), calls=%async_computation.7 | async-start | bytes 1310720 | tf_op jit(solution)/shard_map/reduce_scatter | solution.py:113
  259.2 6.3 %copy-start.3 = (s32[64]{0:T(128)S(1)}, s32[64]{0:T(128)}, u32[]{:S(2)}) copy-start(s32[64]{0:T(128)} %get-tuple-element.335) | copy-start | bytes 772
  259.2 6.5 %copy-start.4 = (u32[32]{0:T(128)S(1)}, u32[32]{0:T(128)}, u32[]{:S(2)}) copy-start(u32[32]{0:T(128)} %constant.146) | copy-start | bytes 388
  265.5 19.1 %copy-start.2 = (bf16[512,128]{1,0:T(8,128)(2,1)S(1)}, bf16[512,128]{1,0:T(8,128)(2,1)}, u32[]{:S(2)}) copy-start(bf16[512,128]{1,0:T(8,128)(2,1)} %param.11) | copy-start | bytes 393220
  274.7 24.2 %copy-start.1 = (f32[1,512]{1,0:T(1,128)}, f32[1,512]{1,0:T(1,128)S(1)}, u32[]{:S(2)}) copy-start(f32[1,512]{1,0:T(1,128)S(1)} %constant_dynamic-slice_fusion.2) | copy-start | bytes 6148
  278.9 12.1 %all-to-all-start.4 = ((f32[8,1,64]{2,1,0:T(1,128)}), f32[8,1,64]{2,1,0:T(1,128)S(1)}, u32[]{:S(2)}, u32[]{:S(2)}) async-start(f32[8,1,64]{2,1,0:T(1,128)} %all_to_all.33), calls=%async_computation.5 | async-start | bytes 8192 | tf_op jit(solution)/shard_map/all_to_all | solution.py:135
  291.6 9.7 %all-to-all-start.5 = ((bf16[32,2,128]{2,1,0:T(2,128)(2,1)}), bf16[32,2,128]{2,1,0:T(2,128)(2,1)S(1)}, u32[]{:S(2)}, u32[]{:S(2)}) async-start(bf16[32,2,128]{2,1,0:T(2,128)(2,1)} %stack.2), calls=%async_computation.6 | async-start | bytes 32768 | tf_op jit(solution)/shard_map/all_to_all | solution.py:152
  303.9 45.5 %all-to-all-start.2 = ((f32[8,64,128]{2,1,0:T(8,128)}), f32[8,64,128]{2,1,0:T(8,128)S(1)}, u32[]{:S(2)}, u32[]{:S(2)}) async-start(f32[8,64,128]{2,1,0:T(8,128)} %bitcast.22), calls=%async_computation.3 | async-start | bytes 524288 | tf_op jit(solution)/shard_map/all_to_all | solution.py:126
Sparse Core Ops, SparseCore 0:
  265.6 25.9 reduce-scatter.1
